TPU v7x, 32 devices: a whole 2x2x4 slice. The times are simulated.
32 devices in a mesh: mode: 8 (over y, x, core), tm: 4 (over z).
Axes of the slice: x: 2, y: 2, z: 4, core: 2. Of those that a mesh axis runs over, the one named last changes fastest.
Arguments:
- field: float32 [2, 128, 65536], P(None, 'mode', 'tm'), may hold values from -1.8 to 1.8
- beta: float32 [3, 128], P(None, 'mode'), may hold values from -1 to 1
- quartets: int32 [4, 1024], replicated, may hold values from 0 to 127
- intersections: float32 [1024], replicated, may hold values from -0.12 to 0.12
Outputs:
- field_out: float32 [2, 128, 65536], P(None, 'mode', 'tm')
- errors: float32 [2, 128], P(None, 'mode')
All inputs are finite; a program needn't handle non-finite values.
Results may differ from a plain program's by a relative error of at most 0.0003.
Values sent between devices are 32-bit elements; how exact they have to be, the bound alone decides.
A program may use at most 128 MiB of HBM per device.

v0:
```python
import math

import jax
import jax.numpy as jnp
from jax import lax
from jax.sharding import PartitionSpec as P

RADIX = 256
STEPS = 2


epsilon = 1e-06


def phase_of(offset, slope, curve, frequency):
    return math.pi * offset + 300.0 * slope * frequency + 3000.0 * curve * frequency * frequency


def triple_product(left_field, middle_field, conj_field):
    prod_re = left_field[0] * middle_field[0] - left_field[1] * middle_field[1]
    prod_im = left_field[0] * middle_field[1] + left_field[1] * middle_field[0]
    out_re = prod_re * conj_field[0] + prod_im * conj_field[1]
    out_im = prod_im * conj_field[0] - prod_re * conj_field[1]
    return (out_re, out_im)


def contract(form, first_operand, second_operand):
    return jnp.einsum(form, first_operand, second_operand, precision=lax.Precision.HIGHEST)


def rotate(real_part, imag_part, angle):
    cosine = jnp.cos(angle)
    sine_part = jnp.sin(angle)
    return (real_part * cosine - imag_part * sine_part, real_part * sine_part + imag_part * cosine)


def dft_tables(length):
    positions = lax.iota(jnp.int32, length)
    product = positions[:, None] * positions[None, :] % length
    angle = -2.0 * math.pi / length * product.astype(jnp.float32)
    return (jnp.cos(angle), jnp.sin(angle))


def to_columns(state):
    return lax.all_to_all(state, "tm", split_axis=3, concat_axis=2, tiled=True)


def to_rows(state):
    return lax.all_to_all(state, "tm", split_axis=2, concat_axis=3, tiled=True)


def linear_step(state, beta, table_re, table_im):
    radix_size = table_re.shape[0]
    total_time = radix_size * radix_size
    cols_local = state.shape[3]
    tm_index = lax.axis_index("tm")
    head_re = contract("ka,mab->mkb", table_re, state[0]) - contract(
        "ka,mab->mkb", table_im, state[1]
    )
    head_im = contract("ka,mab->mkb", table_re, state[1]) + contract(
        "ka,mab->mkb", table_im, state[0]
    )
    column = tm_index * cols_local + lax.iota(jnp.int32, cols_local)
    row_position = lax.iota(jnp.int32, radix_size)
    twist = (
        -2.0
        * math.pi
        / total_time
        * (row_position[:, None] * column[None, :] % total_time).astype(jnp.float32)
    )
    head_re, head_im = rotate(head_re, head_im, twist[None])
    turned = lax.all_to_all(
        jnp.stack([head_re, head_im]), "tm", split_axis=2, concat_axis=3, tiled=True
    )
    spec_re = contract("mcb,kb->mck", turned[0], table_re) - contract(
        "mcb,kb->mck", turned[1], table_im
    )
    spec_im = contract("mcb,kb->mck", turned[1], table_re) + contract(
        "mcb,kb->mck", turned[0], table_im
    )
    rows_local = turned.shape[2]
    first_index = tm_index * rows_local + lax.iota(jnp.int32, rows_local)
    wave = first_index[:, None] + radix_size * row_position[None, :]
    signed = jnp.where(wave < total_time // 2, wave, wave - total_time)
    frequency = signed.astype(jnp.float32) / (total_time / 2)
    angle = phase_of(
        beta[0][:, None, None], beta[1][:, None, None], beta[2][:, None, None], frequency[None]
    )
    spec_re, spec_im = rotate(spec_re, spec_im, angle)
    back_re = contract("mck,kb->mcb", spec_re, table_re) + contract(
        "mck,kb->mcb", spec_im, table_im
    )
    back_im = contract("mck,kb->mcb", spec_im, table_re) - contract(
        "mck,kb->mcb", spec_re, table_im
    )
    untwist = (
        2.0
        * math.pi
        / total_time
        * (first_index[:, None] * row_position[None, :] % total_time).astype(jnp.float32)
    )
    back_re, back_im = rotate(back_re, back_im, untwist[None])
    gathered = lax.all_to_all(
        jnp.stack([back_re, back_im]), "tm", split_axis=3, concat_axis=2, tiled=True
    )
    scale = 1.0 / total_time
    out_re = (
        contract("ka,mkb->mab", table_re, gathered[0])
        + contract("ka,mkb->mab", table_im, gathered[1])
    ) * scale
    out_im = (
        contract("ka,mkb->mab", table_re, gathered[1])
        - contract("ka,mkb->mab", table_im, gathered[0])
    ) * scale
    return jnp.stack([out_re, out_im])


def kerr_term(fields, quartets, intersections):
    count = quartets.shape[1]
    block_size = min(512, count)
    blocks = count // block_size
    grouped = quartets.reshape(4, blocks, block_size).transpose(1, 0, 2)
    weights = intersections.reshape(blocks, block_size)
    modes_all = fields.shape[1]
    mode_ids = lax.iota(jnp.int32, modes_all)

    def accumulate(running, block_item):
        indices, weight = block_item
        out_re, out_im = triple_product(
            jnp.take(fields, indices[1], axis=1),
            jnp.take(fields, indices[2], axis=1),
            jnp.take(fields, indices[3], axis=1),
        )
        owner = (indices[0][None, :] == mode_ids[:, None]).astype(jnp.float32) * weight[None, :]
        add_re = contract("pq,qt->pt", owner, -out_im)
        add_im = contract("pq,qt->pt", owner, out_re)
        return (running + jnp.stack([add_re, add_im]), None)

    running, unused = lax.scan(accumulate, jnp.zeros_like(fields), (grouped, weights))
    return running


def kerr_step(flat, quartets, intersections):
    spread = lax.all_to_all(flat, "mode", split_axis=2, concat_axis=1, tiled=True)
    first = kerr_term(spread, quartets, intersections)
    second = kerr_term(spread + first, quartets, intersections)
    updated = spread + 0.5 * (first + second)
    estimate = 0.5 * (second - first)
    returned, estimate_home = (
        lax.all_to_all(updated, "mode", split_axis=1, concat_axis=2, tiled=True),
        lax.all_to_all(estimate, "mode", split_axis=1, concat_axis=2, tiled=True),
    )
    error_part = jnp.sum(estimate_home * estimate_home, axis=(0, 2))
    field_part = jnp.sum(returned * returned, axis=(0, 2))
    return (returned, error_part, field_part)


def shards(field, beta, quartets, intersections):
    modes_local = field.shape[1]
    time_local = field.shape[2]
    table_re, table_im = dft_tables(RADIX)
    state = field.reshape(2, modes_local, time_local // RADIX, RADIX)
    state = to_columns(state)
    error_rows = []
    for step_index in range(STEPS):
        columns = state
        columns = linear_step(columns, beta, table_re, table_im)
        updated, error_part, field_part = kerr_step(
            columns.reshape(2, modes_local, time_local), quartets, intersections
        )
        error_sq, field_sq = lax.psum((error_part, field_part), "tm")
        error_rows.append(jnp.sqrt(error_sq / (field_sq + epsilon)))
        state = updated.reshape(columns.shape)
    state = to_rows(state)
    errors = jnp.stack(error_rows)
    return (state.reshape(2, modes_local, time_local), errors)


def solution(mesh):
    placed = (P(None, "mode", "tm"), P(None, "mode"), P(), P())
    return jax.shard_map(
        shards,
        mesh=mesh,
        in_specs=placed,
        out_specs=(P(None, "mode", "tm"), P(None, "mode")),
        check_vma=False,
    )
```

profile of v0, /device:TPU:0, one launch (start us, length us, event | category | flops | bytes accessed | tf_op | source)
XLA Modules:
  0.0 1880.1 jit_solution(8491664908036585077)
XLA Ops:
  19.6 47.8 %all-to-all-done = f32[4,1,131072]{2,1,0:T(1,128)S(1)} async-done(((f32[4,1,131072]{2,1,0:T(1,128)}), f32[4,1,131072]{2,1,0:T(1,128)S(1)}, u32[]{:S(2)}, u32[]{:S(2)}) %all-to-all-start) | async-done | bytes 2097184 | tf_op jit(solution)/shard_map/all_to_all | solution.py:45
  110.3 14.0 copy.160
  134.7 47.4 %all-to-all-done.1 = f32[4,1,131072]{2,1,0:T(1,128)} async-done(((f32[4,1,131072]{2,1,0:T(1,128)}), f32[4,1,131072]{2,1,0:T(1,128)}, u32[]{:S(2)}, u32[]{:S(2)}) %all-to-all-start.1) | async-done | bytes 2097184 | tf_op jit(solution)/shard_map/all_to_all | solution.py:72
  235.6 51.0 %all_to_all.174 = f32[4,1,131072]{2,1,0:T(1,128)} all-to-all(f32[4,1,131072]{2,1,0:T(1,128)S(1)} %reshape.495), channel_id=1, replica_groups=mesh['mode'=8,'tm'=4] {'tm'}, dimensions={0} | all-to-all | bytes 4194304 | tf_op jit(solution)/shard_map/all_to_all | solution.py:103
  326.0 14.8 copy.166
  340.9 24.7 %reshape.497 = f32[8,1,65536]{2,1,0:T(1,128)} reshape(f32[16384,2,16]{2,1,0:T(2,128)} %bitcast.446) | data formatting | bytes 4194304
  370.3 26.4 %all-to-all-done.3 = f32[8,1,65536]{2,1,0:T(1,128)} async-done(((f32[8,1,65536]{2,1,0:T(1,128)}), f32[8,1,65536]{2,1,0:T(1,128)}, u32[]{:S(2)}, u32[]{:S(2)}) %all-to-all-start.3) | async-done | bytes 2097184 | tf_op jit(solution)/shard_map/all_to_all | solution.py:144
  403.9 28.6 %reshape.498 = f32[16384,2,16]{2,1,0:T(2,128)} reshape(f32[8,65536]{1,0:T(8,128)S(1)} %reduce.13) | data formatting | bytes 4194304
  432.5 21.6 %copy.201 = f32[2,16,8,2048]{3,1,2,0:T(8,128)} copy(f32[2,16,8,2048]{1,0,3,2:T(2,128)} %bitcast.447) | data formatting | bytes 4194304 | tf_op jit(solution)/shard_map/all_to_all | solution.py:144
  457.3 210.8 %while.44 = (s32[]{:T(128)}, f32[2,128,2048]{2,1,0:T(8,128)}, s32[2,4,512]{2,1,0:T(4,128)S(1)}, f32[2,512]{1,0:T(2,128)S(1)}, f32[2,128,2048]{2,0,1:T(2,128)S(1)}, /*index=5*/s32[]{:T(128)}, s32[]{:T(128)}, s32[]{}, s32[]{}, s32[]{}) while((s32[]{:T(128)}, f32[2,128,2048]{2,1,0:T(8,128)}, s32[2,4,512]{2,1,0:T(4,128)S(1)}, ...), condition=%wide.region_1.3_spmd.clone, body=%wide.region_0.2_spmd.clone.sunk | while | flops 3243000320 | bytes 234956048 | solution.py:139
  457.8 19.4 %gather_fusion = f32[512,2,2048]{2,1,0:T(2,128)} fusion(f32[2,128,2048]{2,0,1:T(2,128)S(1)} %get-tuple-element.665, s32[1024]{0:T(1024)S(1)} %pad_clamp_fusion.24), kind=kCustom, calls=%fused_computation.1.clone.clone.1 | custom fusion | bytes 16779264 | tf_op jit(solution)/shard_map/while/body/eval_jaxpr/jit(_take)/gather | solution.py:131
  489.6 19.5 %gather_fusion.1 = f32[512,2,2048]{2,1,0:T(2,128)} fusion(f32[2,128,2048]{2,0,1:T(2,128)S(1)} %get-tuple-element.665, s32[1024]{0:T(1024)S(1)} %pad_clamp_fusion.25), kind=kCustom, calls=%fused_computation.clone.clone.1 | custom fusion | bytes 16779264 | tf_op jit(solution)/shard_map/while/body/eval_jaxpr/jit(_take)/gather | solution.py:130
  522.6 19.7 %gather_fusion.2 = f32[512,2,2048]{2,1,0:T(2,128)} fusion(f32[2,128,2048]{2,0,1:T(2,128)S(1)} %get-tuple-element.665, s32[1024]{0:T(1024)S(1)} %pad_clamp_fusion.26), kind=kCustom, calls=%fused_computation.2.clone.clone.1 | custom fusion | bytes 16779264 | tf_op jit(solution)/shard_map/while/body/eval_jaxpr/jit(_take)/gather | solution.py:132
  561.5 19.4 %gather_fusion = f32[512,2,2048]{2,1,0:T(2,128)} fusion(f32[2,128,2048]{2,0,1:T(2,128)S(1)} %get-tuple-element.665, s32[1024]{0:T(1024)S(1)} %pad_clamp_fusion.24), kind=kCustom, calls=%fused_computation.1.clone.clone.1 | custom fusion | bytes 16779264 | tf_op jit(solution)/shard_map/while/body/eval_jaxpr/jit(_take)/gather | solution.py:131
  593.3 19.8 %gather_fusion.1 = f32[512,2,2048]{2,1,0:T(2,128)} fusion(f32[2,128,2048]{2,0,1:T(2,128)S(1)} %get-tuple-element.665, s32[1024]{0:T(1024)S(1)} %pad_clamp_fusion.25), kind=kCustom, calls=%fused_computation.clone.clone.1 | custom fusion | bytes 16779264 | tf_op jit(solution)/shard_map/while/body/eval_jaxpr/jit(_take)/gather | solution.py:130
  626.5 19.5 %gather_fusion.2 = f32[512,2,2048]{2,1,0:T(2,128)} fusion(f32[2,128,2048]{2,0,1:T(2,128)S(1)} %get-tuple-element.665, s32[1024]{0:T(1024)S(1)} %pad_clamp_fusion.26), kind=kCustom, calls=%fused_computation.2.clone.clone.1 | custom fusion | bytes 16779264 | tf_op jit(solution)/shard_map/while/body/eval_jaxpr/jit(_take)/gather | solution.py:132
  672.3 215.6 %while.45 = (s32[]{:T(128)}, f32[2,128,2048]{2,1,0:T(8,128)}, s32[2,4,512]{2,1,0:T(4,128)S(1)}, f32[2,512]{1,0:T(2,128)S(1)}, f32[2,128,2048]{2,0,1:T(2,128)S(1)}, /*index=5*/s32[]{:T(128)}, s32[]{:T(128)}, s32[]{}, s32[]{}, s32[]{}) while((s32[]{:T(128)}, f32[2,128,2048]{2,1,0:T(8,128)}, s32[2,4,512]{2,1,0:T(4,128)S(1)}, ...), condition=%wide.region_3.5_spmd.clone, body=%wide.region_2.4_spmd.clone.sunk | while | flops 3243000320 | bytes 234956048 | solution.py:139
  675.7 19.3 %gather_fusion.3 = f32[512,2,2048]{2,1,0:T(2,128)} fusion(f32[2,128,2048]{2,0,1:T(2,128)S(1)} %get-tuple-element.695, s32[1024]{0:T(1024)S(1)} %pad_clamp_fusion.27), kind=kCustom, calls=%fused_computation.4.clone.clone.1 | custom fusion | bytes 16779264 | tf_op jit(solution)/shard_map/while/body/eval_jaxpr/jit(_take)/gather | solution.py:131
  707.5 19.8 %gather_fusion.4 = f32[512,2,2048]{2,1,0:T(2,128)} fusion(f32[2,128,2048]{2,0,1:T(2,128)S(1)} %get-tuple-element.695, s32[1024]{0:T(1024)S(1)} %pad_clamp_fusion.28), kind=kCustom, calls=%fused_computation.3.clone.clone.1 | custom fusion | bytes 16779264 | tf_op jit(solution)/shard_map/while/body/eval_jaxpr/jit(_take)/gather | solution.py:130
  740.7 19.5 %gather_fusion.5 = f32[512,2,2048]{2,1,0:T(2,128)} fusion(f32[2,128,2048]{2,0,1:T(2,128)S(1)} %get-tuple-element.695, s32[1024]{0:T(1024)S(1)} %pad_clamp_fusion.29), kind=kCustom, calls=%fused_computation.5.clone.clone.1 | custom fusion | bytes 16779264 | tf_op jit(solution)/shard_map/while/body/eval_jaxpr/jit(_take)/gather | solution.py:132
  779.7 19.4 %gather_fusion.3 = f32[512,2,2048]{2,1,0:T(2,128)} fusion(f32[2,128,2048]{2,0,1:T(2,128)S(1)} %get-tuple-element.695, s32[1024]{0:T(1024)S(1)} %pad_clamp_fusion.27), kind=kCustom, calls=%fused_computation.4.clone.clone.1 | custom fusion | bytes 16779264 | tf_op jit(solution)/shard_map/while/body/eval_jaxpr/jit(_take)/gather | solution.py:131
  811.4 19.5 %gather_fusion.4 = f32[512,2,2048]{2,1,0:T(2,128)} fusion(f32[2,128,2048]{2,0,1:T(2,128)S(1)} %get-tuple-element.695, s32[1024]{0:T(1024)S(1)} %pad_clamp_fusion.28), kind=kCustom, calls=%fused_computation.3.clone.clone.1 | custom fusion | bytes 16779264 | tf_op jit(solution)/shard_map/while/body/eval_jaxpr/jit(_take)/gather | solution.py:130
  844.4 19.7 %gather_fusion.5 = f32[512,2,2048]{2,1,0:T(2,128)} fusion(f32[2,128,2048]{2,0,1:T(2,128)S(1)} %get-tuple-element.695, s32[1024]{0:T(1024)S(1)} %pad_clamp_fusion.29), kind=kCustom, calls=%fused_computation.5.clone.clone.1 | custom fusion | bytes 16779264 | tf_op jit(solution)/shard_map/while/body/eval_jaxpr/jit(_take)/gather | solution.py:132
  894.5 29.0 %all_to_all.175 = f32[2,128,2048]{2,0,1:T(2,128)S(1)} all-to-all(f32[2,128,2048]{2,0,1:T(2,128)S(1)} %copy.171), channel_id=1, replica_groups=mesh['mode'=8,'tm'=4] {'mode'}, dimensions={1} | all-to-all | bytes 4194304 | tf_op jit(solution)/shard_map/all_to_all | solution.py:150
  960.9 51.2 %all_to_all.176 = f32[4,1,131072]{2,1,0:T(1,128)} all-to-all(f32[4,1,131072]{2,1,0:T(1,128)S(1)} %reshape.499), channel_id=1, replica_groups=mesh['mode'=8,'tm'=4] {'tm'}, dimensions={0} | all-to-all | bytes 4194304 | tf_op jit(solution)/shard_map/all_to_all | solution.py:72
  1065.7 50.5 %all_to_all.177 = f32[4,1,131072]{2,1,0:T(1,128)} all-to-all(f32[4,1,131072]{2,1,0:T(1,128)S(1)} %reshape.501), channel_id=1, replica_groups=mesh['mode'=8,'tm'=4] {'tm'}, dimensions={0} | all-to-all | bytes 4194304 | tf_op jit(solution)/shard_map/all_to_all | solution.py:103
  1155.3 14.8 copy.183
  1170.0 24.8 %reshape.503 = f32[8,1,65536]{2,1,0:T(1,128)} reshape(f32[16384,2,16]{2,1,0:T(2,128)} %bitcast.448) | data formatting | bytes 4194304
  1202.3 23.6 %all-to-all-done.7 = f32[8,1,65536]{2,1,0:T(1,128)} async-done(((f32[8,1,65536]{2,1,0:T(1,128)}), f32[8,1,65536]{2,1,0:T(1,128)}, u32[]{:S(2)}, u32[]{:S(2)}) %all-to-all-start.7) | async-done | bytes 2097184 | tf_op jit(solution)/shard_map/all_to_all | solution.py:144
  1237.9 28.7 %reshape.504 = f32[16384,2,16]{2,1,0:T(2,128)} reshape(f32[8,65536]{1,0:T(8,128)S(1)} %reduce.16) | data formatting | bytes 4194304
  1266.6 21.6 %copy.203 = f32[2,16,8,2048]{3,1,2,0:T(8,128)} copy(f32[2,16,8,2048]{1,0,3,2:T(2,128)} %bitcast.449) | data formatting | bytes 4194304 | tf_op jit(solution)/shard_map/all_to_all | solution.py:144
  1291.4 210.6 %while.46 = (s32[]{:T(128)}, f32[2,128,2048]{2,1,0:T(8,128)}, s32[2,4,512]{2,1,0:T(4,128)S(1)}, f32[2,512]{1,0:T(2,128)S(1)}, f32[2,128,2048]{2,0,1:T(2,128)S(1)}, /*index=5*/s32[]{:T(128)}, s32[]{:T(128)}, s32[]{}, s32[]{}, s32[]{}) while((s32[]{:T(128)}, f32[2,128,2048]{2,1,0:T(8,128)}, s32[2,4,512]{2,1,0:T(4,128)S(1)}, ...), condition=%wide.region_5.7_spmd.clone, body=%wide.region_4.6_spmd.clone.sunk | while | flops 3243000320 | bytes 234956048 | solution.py:139
  1291.7 19.3 %gather_fusion.6 = f32[512,2,2048]{2,1,0:T(2,128)} fusion(f32[2,128,2048]{2,0,1:T(2,128)S(1)} %get-tuple-element.725, s32[1024]{0:T(1024)S(1)} %pad_clamp_fusion.30), kind=kCustom, calls=%fused_computation.7.clone.clone.1 | custom fusion | bytes 16779264 | tf_op jit(solution)/shard_map/while/body/eval_jaxpr/jit(_take)/gather | solution.py:131
  1323.5 19.8 %gather_fusion.7 = f32[512,2,2048]{2,1,0:T(2,128)} fusion(f32[2,128,2048]{2,0,1:T(2,128)S(1)} %get-tuple-element.725, s32[1024]{0:T(1024)S(1)} %pad_clamp_fusion.31), kind=kCustom, calls=%fused_computation.6.clone.clone.1 | custom fusion | bytes 16779264 | tf_op jit(solution)/shard_map/while/body/eval_jaxpr/jit(_take)/gather | solution.py:130
  1356.7 19.5 %gather_fusion.8 = f32[512,2,2048]{2,1,0:T(2,128)} fusion(f32[2,128,2048]{2,0,1:T(2,128)S(1)} %get-tuple-element.725, s32[1024]{0:T(1024)S(1)} %pad_clamp_fusion.32), kind=kCustom, calls=%fused_computation.8.clone.clone.1 | custom fusion | bytes 16779264 | tf_op jit(solution)/shard_map/while/body/eval_jaxpr/jit(_take)/gather | solution.py:132
  1395.7 19.3 %gather_fusion.6 = f32[512,2,2048]{2,1,0:T(2,128)} fusion(f32[2,128,2048]{2,0,1:T(2,128)S(1)} %get-tuple-element.725, s32[1024]{0:T(1024)S(1)} %pad_clamp_fusion.30), kind=kCustom, calls=%fused_computation.7.clone.clone.1 | custom fusion | bytes 16779264 | tf_op jit(solution)/shard_map/while/body/eval_jaxpr/jit(_take)/gather | solution.py:131
  1415.0 12.4 fusion.490
  1427.5 19.5 %gather_fusion.7 = f32[512,2,2048]{2,1,0:T(2,128)} fusion(f32[2,128,2048]{2,0,1:T(2,128)S(1)} %get-tuple-element.725, s32[1024]{0:T(1024)S(1)} %pad_clamp_fusion.31), kind=kCustom, calls=%fused_computation.6.clone.clone.1 | custom fusion | bytes 16779264 | tf_op jit(solution)/shard_map/while/body/eval_jaxpr/jit(_take)/gather | solution.py:130
  1460.4 19.7 %gather_fusion.8 = f32[512,2,2048]{2,1,0:T(2,128)} fusion(f32[2,128,2048]{2,0,1:T(2,128)S(1)} %get-tuple-element.725, s32[1024]{0:T(1024)S(1)} %pad_clamp_fusion.32), kind=kCustom, calls=%fused_computation.8.clone.clone.1 | custom fusion | bytes 16779264 | tf_op jit(solution)/shard_map/while/body/eval_jaxpr/jit(_take)/gather | solution.py:132
  1506.2 229.3 %while.47 = (s32[]{:T(128)}, f32[2,128,2048]{2,1,0:T(8,128)}, s32[2,4,512]{2,1,0:T(4,128)S(1)}, f32[2,512]{1,0:T(2,128)S(1)}, f32[2,128,2048]{2,0,1:T(2,128)S(1)}, /*index=5*/s32[]{:T(128)}, s32[]{:T(128)}, s32[]{}, s32[]{}, s32[]{}) while((s32[]{:T(128)}, f32[2,128,2048]{2,1,0:T(8,128)}, s32[2,4,512]{2,1,0:T(4,128)S(1)}, ...), condition=%wide.region_7.9_spmd.clone, body=%wide.region_6.8_spmd.clone.sunk | while | flops 3243000320 | bytes 234956048 | solution.py:139
  1509.7 19.3 %gather_fusion.9 = f32[512,2,2048]{2,1,0:T(2,128)} fusion(f32[2,128,2048]{2,0,1:T(2,128)S(1)} %get-tuple-element.755, s32[1024]{0:T(1024)S(1)} %pad_clamp_fusion.33), kind=kCustom, calls=%fused_computation.10.clone.clone.1 | custom fusion | bytes 16779264 | tf_op jit(solution)/shard_map/while/body/eval_jaxpr/jit(_take)/gather | solution.py:131
  1541.5 30.0 %gather_fusion.10 = f32[512,2,2048]{2,1,0:T(2,128)} fusion(f32[2,128,2048]{2,0,1:T(2,128)S(1)} %get-tuple-element.755, s32[1024]{0:T(1024)S(1)} %pad_clamp_fusion.34), kind=kCustom, calls=%fused_computation.9.clone.clone.1 | custom fusion | bytes 16779264 | tf_op jit(solution)/shard_map/while/body/eval_jaxpr/jit(_take)/gather | solution.py:130
  1584.9 19.7 %gather_fusion.11 = f32[512,2,2048]{2,1,0:T(2,128)} fusion(f32[2,128,2048]{2,0,1:T(2,128)S(1)} %get-tuple-element.755, s32[1024]{0:T(1024)S(1)} %pad_clamp_fusion.35), kind=kCustom, calls=%fused_computation.11.clone.clone.1 | custom fusion | bytes 16779264 | tf_op jit(solution)/shard_map/while/body/eval_jaxpr/jit(_take)/gather | solution.py:132
  1623.8 19.3 %gather_fusion.9 = f32[512,2,2048]{2,1,0:T(2,128)} fusion(f32[2,128,2048]{2,0,1:T(2,128)S(1)} %get-tuple-element.755, s32[1024]{0:T(1024)S(1)} %pad_clamp_fusion.33), kind=kCustom, calls=%fused_computation.10.clone.clone.1 | custom fusion | bytes 16779264 | tf_op jit(solution)/shard_map/while/body/eval_jaxpr/jit(_take)/gather | solution.py:131
  1655.6 19.7 %gather_fusion.10 = f32[512,2,2048]{2,1,0:T(2,128)} fusion(f32[2,128,2048]{2,0,1:T(2,128)S(1)} %get-tuple-element.755, s32[1024]{0:T(1024)S(1)} %pad_clamp_fusion.34), kind=kCustom, calls=%fused_computation.9.clone.clone.1 | custom fusion | bytes 16779264 | tf_op jit(solution)/shard_map/while/body/eval_jaxpr/jit(_take)/gather | solution.py:130
  1688.7 19.5 %gather_fusion.11 = f32[512,2,2048]{2,1,0:T(2,128)} fusion(f32[2,128,2048]{2,0,1:T(2,128)S(1)} %get-tuple-element.755, s32[1024]{0:T(1024)S(1)} %pad_clamp_fusion.35), kind=kCustom, calls=%fused_computation.11.clone.clone.1 | custom fusion | bytes 16779264 | tf_op jit(solution)/shard_map/while/body/eval_jaxpr/jit(_take)/gather | solution.py:132
  1752.0 22.1 %all-to-all-done.8 = f32[2,128,2048]{2,0,1:T(2,128)S(1)} async-done(((f32[2,128,2048]{2,0,1:T(2,128)}), f32[2,128,2048]{2,0,1:T(2,128)S(1)}, u32[]{:S(2)}, u32[]{:S(2)}) %all-to-all-start.8) | async-done | bytes 2097184 | tf_op jit(solution)/shard_map/all_to_all | solution.py:150
  1819.6 27.5 %all-reduce = (f32[16]{0:T(128)S(1)}, f32[16]{0:T(128)S(1)}, f32[16]{0:T(128)S(1)}, f32[16]{0:T(128)S(1)}) all-reduce(f32[16]{0:T(128)S(1)} %reduce_sum.56, f32[16]{0:T(128)S(1)} %multiply_reduce_fusion, f32[16]{0:T(128)S(1)} %reduce_sum.52, f32[16]{0:T(128)S(1)} %multiply_reduce_fusion.2), channel_id=1, replica_groups=mesh['mode'=8,'tm'=4] {'tm'}, use_global_device_ids=true, to_apply=%region_15.17 | all-reduce | flops 64 | bytes 512 | tf_op jit(solution)/shard_map/psum | solution.py:171
  (380 shorter events, 790.7 us)
Async XLA Ops:
  12.9 54.5 %all-to-all-start = ((f32[4,1,131072]{2,1,0:T(1,128)}), f32[4,1,131072]{2,1,0:T(1,128)S(1)}, u32[]{:S(2)}, u32[]{:S(2)}) async-start(f32[4,1,131072]{2,1,0:T(1,128)} %reshape.491), calls=%async_computation | async-start | bytes 4194304 | tf_op jit(solution)/shard_map/all_to_all | solution.py:45
  19.6 90.0 %copy-start.27 = (f32[256,64]{0,1:T(8,128)}, f32[256,64]{0,1:T(8,128)S(1)}, u32[]{:S(2)}) copy-start(f32[256,64]{0,1:T(8,128)S(1)} %get-tuple-element.433) | copy-start | bytes 196612
  19.6 90.0 %copy-start.29 = (f32[256,64]{0,1:T(8,128)}, f32[256,64]{0,1:T(8,128)S(1)}, u32[]{:S(2)}) copy-start(f32[256,64]{0,1:T(8,128)S(1)} %get-tuple-element.434) | copy-start | bytes 196612
  124.3 10.0 copy-start.40
  129.8 52.3 %all-to-all-start.1 = ((f32[4,1,131072]{2,1,0:T(1,128)}), f32[4,1,131072]{2,1,0:T(1,128)}, u32[]{:S(2)}, u32[]{:S(2)}) async-start(f32[4,1,131072]{2,1,0:T(1,128)} %reshape.493), calls=%async_computation.1 | async-start | bytes 4194304 | tf_op jit(solution)/shard_map/all_to_all | solution.py:72
  134.3 78.0 %copy-start.33 = (f32[16]{0:T(128)}, f32[16]{0:T(128)S(1)}, u32[]{:S(2)}) copy-start(f32[16]{0:T(128)S(1)} %get-tuple-element.427) | copy-start | bytes 196
  134.3 78.0 %copy-start.35 = (f32[16]{0:T(128)}, f32[16]{0:T(128)S(1)}, u32[]{:S(2)}) copy-start(f32[16]{0:T(128)S(1)} %get-tuple-element.428) | copy-start | bytes 196
  134.3 78.0 %copy-start.37 = (f32[16]{0:T(128)}, f32[16]{0:T(128)S(1)}, u32[]{:S(2)}) copy-start(f32[16]{0:T(128)S(1)} %get-tuple-element.429) | copy-start | bytes 196
  134.7 77.6 %copy-start.25 = (f32[64,256]{1,0:T(8,128)}, f32[64,256]{1,0:T(8,128)S(1)}, u32[]{:S(2)}) copy-start(f32[64,256]{1,0:T(8,128)S(1)} %get-tuple-element.432) | copy-start | bytes 196612
  134.7 89.5 %copy-start.21 = (f32[64,256]{1,0:T(8,128)}, f32[64,256]{1,0:T(8,128)S(1)}, u32[]{:S(2)}) copy-start(f32[64,256]{1,0:T(8,128)S(1)} %get-tuple-element.430) | copy-start | bytes 196612
  134.7 89.5 %copy-start.23 = (f32[64,256]{1,0:T(8,128)}, f32[64,256]{1,0:T(8,128)S(1)}, u32[]{:S(2)}) copy-start(f32[64,256]{1,0:T(8,128)S(1)} %get-tuple-element.431) | copy-start | bytes 196612
  365.6 31.1 %all-to-all-start.3 = ((f32[8,1,65536]{2,1,0:T(1,128)}), f32[8,1,65536]{2,1,0:T(1,128)}, u32[]{:S(2)}, u32[]{:S(2)}) async-start(f32[8,1,65536]{2,1,0:T(1,128)} %reshape.497), calls=%async_computation.3 | async-start | bytes 4194304 | tf_op jit(solution)/shard_map/all_to_all | solution.py:144
  509.1 9.2 copy-start.8
  542.3 9.2 copy-start
  542.3 9.2 copy-start.1
  613.1 9.2 copy-start.8
  646.0 9.2 copy-start
  646.0 9.2 copy-start.1
  727.3 9.2 copy-start.9
  760.2 9.2 copy-start.2
  760.2 9.2 copy-start.3
  830.9 9.2 copy-start.9
  864.1 9.2 copy-start.2
  864.1 9.2 copy-start.3
  935.7 11.7 copy-start.28
  935.7 11.7 copy-start.30
  1035.4 6.9 copy-start.26
  1035.5 6.9 copy-start.34
  1035.5 6.9 copy-start.36
  1035.5 6.9 copy-start.38
  1194.8 31.1 %all-to-all-start.7 = ((f32[8,1,65536]{2,1,0:T(1,128)}), f32[8,1,65536]{2,1,0:T(1,128)}, u32[]{:S(2)}, u32[]{:S(2)}) async-start(f32[8,1,65536]{2,1,0:T(1,128)} %reshape.503), calls=%async_computation.7 | async-start | bytes 4194304 | tf_op jit(solution)/shard_map/all_to_all | solution.py:144
  1225.9 517.5 %all-to-all-start.10 = ((f32[2,128,2048]{2,0,1:T(2,128)}), f32[2,128,2048]{2,0,1:T(2,128)}, u32[]{:S(2)}, u32[]{:S(2)}) async-start(f32[2,128,2048]{2,0,1:T(2,128)} %copy.193), calls=%async_computation.10 | async-start | bytes 4194304 | tf_op jit(solution)/shard_map/all_to_all | solution.py:151
  1343.3 9.2 copy-start.10
  1376.2 9.2 copy-start.4
  1376.2 9.2 copy-start.5
  1447.0 9.2 copy-start.10
  1480.1 9.2 copy-start.4
  1480.1 9.2 copy-start.5
  1571.5 9.2 copy-start.11
  1604.6 9.2 copy-start.6
  1604.6 9.2 copy-start.7
  1675.3 9.2 copy-start.11
  1708.2 9.2 copy-start.6
  1708.2 9.2 copy-start.7
  1743.4 30.7 %all-to-all-start.8 = ((f32[2,128,2048]{2,0,1:T(2,128)}), f32[2,128,2048]{2,0,1:T(2,128)S(1)}, u32[]{:S(2)}, u32[]{:S(2)}) async-start(f32[2,128,2048]{2,0,1:T(2,128)} %copy.188), calls=%async_computation.8 | async-start | bytes 4194304 | tf_op jit(solution)/shard_map/all_to_all | solution.py:150
  1774.1 31.0 %all-to-all-start.11 = ((f32[2,128,2048]{2,0,1:T(2,128)}), f32[2,128,2048]{2,0,1:T(2,128)}, u32[]{:S(2)}, u32[]{:S(2)}) async-start(f32[2,128,2048]{2,0,1:T(2,128)} %copy.194), calls=%async_computation.11 | async-start | bytes 4194304 | tf_op jit(solution)/shard_map/all_to_all | solution.py:151
  1798.0 14.8 copy-start.14
  1805.1 50.5 %all-to-all-start.9 = ((f32[4,1,131072]{2,1,0:T(1,128)}), f32[4,1,131072]{2,1,0:T(1,128)}, u32[]{:S(2)}, u32[]{:S(2)}) async-start(f32[4,1,131072]{2,1,0:T(1,128)} %reshape.505), calls=%async_computation.9 | async-start | bytes 4194304 | tf_op jit(solution)/shard_map/all_to_all | solution.py:49
  (13 other events, 57.8 us)
where the time goes:
time: 1900 us; the launch traced here: 1880 us
  local copies, waits for them, and re-layouts  878 us (46%)
  other arithmetic  397 us (21%)
  blocking collectives  209 us (11%)
  waiting for transfers between devices  182 us (10%)
  matrix products  148 us (8%)
  starting transfers between devices  37.8 us (2%)
  loops' own time  25.8 us (1%)
    unnamed x79, local copies, waits for them, and re-layouts  174 us
    gather x8, local copies, waits for them, and re-layouts, accumulate(): jnp.take(fields, indices[1], axis=1)  168 us
    gather x8, local copies, waits for them, and re-layouts, accumulate(): jnp.take(fields, indices[3], axis=1)  157 us
    gather x8, local copies, waits for them, and re-layouts, accumulate(): jnp.take(fields, indices[2], axis=1)  155 us
    dot_general x44, matrix products, contract(): jnp.einsum(form, first_operand, second_operand, precision=lax.Precision.H...  138 us
    all_to_all x2, blocking collectives, linear_step(): lax.all_to_all(jnp.stack([back_re, back_im]), 'tm', split_axis=3, concat_...  101 us
    select_n x8, other arithmetic, accumulate(): jnp.take(fields, indices[2], axis=1)  99.3 us
    select_n x16, other arithmetic, accumulate(): jnp.take(fields, indices[3], axis=1)  73.6 us
  transfers between devices with their start and end apart: 8, of which 7 were waited for; matrix products, arithmetic and copies ran while one was open for 29% of the time, Pallas kernels for 0%

commit v1 on v0

--- a/solution.py
+++ b/solution.py
@@ -1,8 +1,11 @@
+import functools
 import math
 
 import jax
 import jax.numpy as jnp
 from jax import lax
+from jax.experimental import pallas as pl
+from jax.experimental.pallas import tpu as pltpu
 from jax.sharding import PartitionSpec as P
 
 RADIX = 256
@@ -155,7 +158,7 @@
     return (returned, error_part, field_part)
 
 
-def shards(field, beta, quartets, intersections):
+def shards_general(field, beta, quartets, intersections):
     modes_local = field.shape[1]
     time_local = field.shape[2]
     table_re, table_im = dft_tables(RADIX)
@@ -176,10 +179,203 @@
     return (state.reshape(2, modes_local, time_local), errors)
 
 
+UNROLL = 8
+
+
+def split(value):
+    high = value.astype(jnp.bfloat16)
+    low = (value - high.astype(jnp.float32)).astype(jnp.bfloat16)
+    return high, low
+
+
+def split_table(value):
+    high = lax.reduce_precision(value, exponent_bits=8, mantissa_bits=7)
+    return high.astype(jnp.bfloat16), (value - high).astype(jnp.bfloat16)
+
+
+def product(left, right):
+    dot = lambda a, b: jnp.dot(a, b, preferred_element_type=jnp.float32)
+    return dot(left[0], right[0]) + (dot(left[0], right[1]) + dot(left[1], right[0]))
+
+
+def spectral_kernel(x_ref, m1h, m1l, m2h, m2l, twist_ref, rotor_ref, out_ref):
+    radix = twist_ref.shape[1]
+    m1 = (m1h[...], m1l[...])
+    m2 = (m2h[...], m2l[...])
+    real = x_ref[:, 0, 0].reshape(radix, radix)
+    imag = x_ref[:, 1, 0].reshape(radix, radix)
+    head = product(m1, split(jnp.concatenate([real, imag], axis=0)))
+    head_re, head_im = head[:radix], head[radix:]
+    tw_re, tw_im = twist_ref[0], twist_ref[1]
+    re = head_re * tw_re - head_im * tw_im
+    im = head_re * tw_im + head_im * tw_re
+    spec = product(split(jnp.concatenate([re, im], axis=1)), m2)
+    spec_re, spec_im = spec[:, :radix], spec[:, radix:]
+    ro_re, ro_im = rotor_ref[0, 0], rotor_ref[1, 0]
+    re = spec_re * ro_re - spec_im * ro_im
+    im = spec_re * ro_im + spec_im * ro_re
+    back = product(split(jnp.concatenate([re, im], axis=1)), m1)
+    back_re, back_im = back[:, :radix], back[:, radix:]
+    re = back_re * tw_re + back_im * tw_im
+    im = back_im * tw_re - back_re * tw_im
+    out = product(m2, split(jnp.concatenate([re, im], axis=0)))
+    shape = out_ref.shape[:1] + out_ref.shape[3:]
+    out_ref[:, 0, 0] = out[:radix].reshape(shape)
+    out_ref[:, 1, 0] = out[radix:].reshape(shape)
+
+
+def spectral(x, tables, twist, rotor, blocks):
+    count, _, modes, rows, radix = x.shape
+    whole = lambda a: pl.BlockSpec(a.shape, lambda g: (0,) * a.ndim)
+    return pl.pallas_call(
+        spectral_kernel,
+        grid=(modes,),
+        in_specs=[pl.BlockSpec((count, 2, 1, rows, radix), lambda g: (0, 0, g, 0, 0))]
+        + [whole(t) for t in tables]
+        + [whole(twist), pl.BlockSpec((2, 1, radix, radix), lambda g: (0, g, 0, 0))],
+        out_specs=pl.BlockSpec((blocks, 2, 1, radix // blocks, radix), lambda g: (0, 0, g, 0, 0)),
+        out_shape=jax.ShapeDtypeStruct((blocks, 2, modes, radix // blocks, radix), jnp.float32),
+        compiler_params=pltpu.CompilerParams(vmem_limit_bytes=48 * 1024 * 1024),
+        name="spectral",
+    )(x, *tables, twist, rotor)
+
+
+def kerr_kernel(stride, quartets, weights, lin_ref, out_ref, err_ref, first_ref, acc_ref, mid_ref):
+    count = quartets.shape[1]
+    unroll = UNROLL if count % UNROLL == 0 else 1
+
+    def evaluate(src, dst):
+        dst[...] = jnp.zeros_like(dst)
+
+        def chunk(c, carry):
+            pending = []
+            for u in range(unroll):
+                q = c * unroll + u
+                l, m, n = quartets[1, q], quartets[2, q], quartets[3, q]
+                w = weights[q]
+                re, im = triple_product(
+                    (src[l], src[l + stride]), (src[m], src[m + stride]), (src[n], src[n + stride])
+                )
+                pending.append((quartets[0, q], -w * im, w * re))
+            for p, re, im in pending:
+                dst[p] += re
+                dst[p + stride] += im
+            return carry
+
+        lax.fori_loop(0, count // unroll, chunk, 0)
+
+    evaluate(lin_ref, first_ref)
+    mid_ref[...] = lin_ref[...] + first_ref[...]
+    evaluate(mid_ref, acc_ref)
+
+    def finish(i, carry):
+        first, second = first_ref[i], acc_ref[i]
+        new = lin_ref[i] + 0.5 * (first + second)
+        estimate = 0.5 * (second - first)
+        out_ref[i] = new
+        err_ref[0, pl.ds(i, 1)] = jnp.sum(estimate * estimate, axis=0, keepdims=True)
+        err_ref[1, pl.ds(i, 1)] = jnp.sum(new * new, axis=0, keepdims=True)
+        return carry
+
+    lax.fori_loop(0, lin_ref.shape[0], finish, 0, unroll=4)
+
+
+def kerr(lin, quartets, weights, stride):
+    planes, rows, lanes = lin.shape
+    vmem = pl.BlockSpec(memory_space=pltpu.VMEM)
+    smem = pl.BlockSpec(memory_space=pltpu.SMEM)
+    return pl.pallas_call(
+        functools.partial(kerr_kernel, stride),
+        in_specs=[smem, smem, vmem],
+        out_specs=[vmem, vmem],
+        out_shape=[
+            jax.ShapeDtypeStruct(lin.shape, jnp.float32),
+            jax.ShapeDtypeStruct((2, planes, lanes), jnp.float32),
+        ],
+        scratch_shapes=[pltpu.VMEM(lin.shape, jnp.float32)] * 3,
+        compiler_params=pltpu.CompilerParams(vmem_limit_bytes=40 * 1024 * 1024),
+        name="kerr",
+    )(quartets, weights, lin)
+
+
+def shards(ways, field, beta, quartets, intersections):
+    mode_ways, tm_ways = ways
+    devices = mode_ways * tm_ways
+    _, modes_local, time_local = field.shape
+    total_time = time_local * tm_ways
+    radix = math.isqrt(total_time)
+    own = modes_local // tm_ways
+    modes_all = modes_local * mode_ways
+    rows = radix // devices
+    tm_index = lax.axis_index("tm")
+    mode_index = lax.axis_index("mode")
+
+    table_re, table_im = dft_tables(radix)
+    m1 = jnp.concatenate(
+        [jnp.concatenate([table_re, -table_im], 1), jnp.concatenate([table_im, table_re], 1)], 0
+    )
+    m2 = jnp.concatenate(
+        [jnp.concatenate([table_re, table_im], 1), jnp.concatenate([-table_im, table_re], 1)], 0
+    )
+    tables = split_table(m1) + split_table(m2)
+    position = lax.iota(jnp.int32, radix)
+    angle = (
+        -2.0
+        * math.pi
+        / total_time
+        * (position[:, None] * position[None, :] % total_time).astype(jnp.float32)
+    )
+    twist = jnp.stack([jnp.cos(angle), jnp.sin(angle)])
+    wave = position[:, None] + radix * position[None, :]
+    signed = jnp.where(wave < total_time // 2, wave, wave - total_time)
+    frequency = signed.astype(jnp.float32) / (total_time / 2)
+    mine = lax.dynamic_slice_in_dim(beta, tm_index * own, own, axis=1)
+    phase = phase_of(
+        mine[0][:, None, None], mine[1][:, None, None], mine[2][:, None, None], frequency[None]
+    )
+    rotor = jnp.stack([jnp.cos(phase), jnp.sin(phase)]) * (1.0 / total_time)
+
+    holder = quartets % modes_local // own * mode_ways + quartets // modes_local
+    planes = holder * (2 * own) + quartets % own
+
+    state = field.reshape(2, tm_ways, own, time_local // radix, radix).transpose(1, 0, 2, 3, 4)
+    state = lax.all_to_all(state, "tm", split_axis=0, concat_axis=0, tiled=True)
+    sums = []
+    for step_index in range(STEPS):
+        state = spectral(state, tables, twist, rotor, devices)
+        state = lax.all_to_all(state, ("tm", "mode"), split_axis=0, concat_axis=0, tiled=True)
+        flat, part = kerr(
+            state.reshape(2 * modes_all, rows, radix), planes, intersections, own
+        )
+        sums.append(part)
+        state = flat.reshape(devices, 2, own, rows, radix)
+        if step_index < STEPS - 1:
+            state = lax.all_to_all(state, ("tm", "mode"), split_axis=0, concat_axis=0, tiled=True)
+    state = state.reshape(tm_ways, mode_ways, 2, own, rows, radix)
+    state = lax.all_to_all(state, "mode", split_axis=1, concat_axis=1, tiled=True)
+    out = state.transpose(2, 0, 3, 1, 4, 5).reshape(2, modes_local, time_local)
+
+    norms = jnp.sum(jnp.stack(sums), axis=-1).reshape(STEPS, 2, tm_ways, mode_ways, 2, own)
+    norms = jnp.sum(norms, axis=4)
+    norms = lax.psum(norms, ("mode", "tm"))
+    norms = lax.dynamic_index_in_dim(norms, mode_index, axis=3, keepdims=False)
+    norms = norms.reshape(STEPS, 2, modes_local)
+    errors = jnp.sqrt(norms[:, 0] / (norms[:, 1] + epsilon))
+    return (out, errors)
+
+
 def solution(mesh):
     placed = (P(None, "mode", "tm"), P(None, "mode"), P(), P())
+
+    def body(field, beta, quartets, intersections):
+        mode_ways, tm_ways = mesh.shape["mode"], mesh.shape["tm"]
+        devices = mode_ways * tm_ways
+        if field.shape[1] % tm_ways == 0 and RADIX % (8 * devices) == 0:
+            return shards((mode_ways, tm_ways), field, beta, quartets, intersections)
+        return shards_general(field, beta, quartets, intersections)
+
     return jax.shard_map(
-        shards,
+        body,
         mesh=mesh,
         in_specs=placed,
         out_specs=(P(None, "mode", "tm"), P(None, "mode")),

time: 1900 us -> 354 us (0.19); the launches traced: 1880 us -> 354 us
  local copies, waits for them, and re-layouts: 878 us -> 10.9 us
  other arithmetic: 397 us -> 9.76 us
  matrix products: 148 us -> 0 us
  waiting for transfers between devices: 182 us -> 88.1 us
  Pallas kernels: 0 us -> 68.1 us
  blocking collectives: 209 us -> 162 us
  loops' own time: 25.8 us -> 0 us
  starting transfers between devices: 37.8 us -> 13.9 us
    gather x24 -> x0, local copies, waits for them, and re-layouts: 479 us -> none  [the longest x8 168 us: accumulate(): jnp.take(fields, indices[1], axis=1)]
    select_n x40 -> x0, other arithmetic: 246 us -> none  [the longest x8 99.3 us: accumulate(): jnp.take(fields, indices[2], axis=1)]
    unnamed x79 -> x23, local copies, waits for them, and re-layouts: 174 us -> 3.08 us
    dot_general x44 -> x0, matrix products: 138 us -> none  [contract(): jnp.einsum(form, first_operand, second_operand, precision=lax.Precision.H...]
    all_to_all x8 -> x3, waiting for transfers between devices: 182 us -> 88.1 us  [the longest x1 48.7 us: shards(): lax.all_to_all(state, ('tm', 'mode'), split_axis=0, concat_axis=0, tiled=...]
    all_to_all x11 -> x0, local copies, waits for them, and re-layouts: 79.2 us -> none  [the longest x2 43.2 us: kerr_step(): lax.all_to_all(flat, 'mode', split_axis=2, concat_axis=1, tiled=True)]
    all_to_all x4 -> x2, blocking collectives: 182 us -> 105 us  [shards(): lax.all_to_all(state, ('tm', 'mode'), split_axis=0, concat_axis=0, tiled=...]
    pallas_call x0 -> x4, Pallas kernels: none -> 68.1 us  [the longest x2 41.1 us: kerr(): pl.pallas_call(functools.partial(kerr_kernel, stride), in_specs=[smem, sm...]
  transfers between devices with their start and end apart: 8 -> 3, of which waited for: 7 -> 2; matrix products, arithmetic and copies ran while one was open for 29% -> 3% of each run, Pallas kernels for 0% -> 0%
where the time goes in v1:
time: 354 us
  blocking collectives  162 us (46%)
  waiting for transfers between devices  88.1 us (25%)
  Pallas kernels  68.1 us (19%)
  starting transfers between devices  13.9 us (4%)
  local copies, waits for them, and re-layouts  10.9 us (3%)
  other arithmetic  9.76 us (3%)
    all_to_all x2, blocking collectives, shards(): lax.all_to_all(state, ('tm', 'mode'), split_axis=0, concat_axis=0, tiled=...  105 us
    psum x1, blocking collectives, shards(): norms = lax.psum(norms, ('mode', 'tm'))  57.4 us
    all_to_all x1, waiting for transfers between devices, shards(): lax.all_to_all(state, ('tm', 'mode'), split_axis=0, concat_axis=0, tiled=...  48.7 us
    pallas_call x2, Pallas kernels, kerr(): pl.pallas_call(functools.partial(kerr_kernel, stride), in_specs=[smem, sm...  41.1 us
    all_to_all x1, waiting for transfers between devices, shards(): state = lax.all_to_all(state, 'tm', split_axis=0, concat_axis=0, tiled=True)  39.4 us
    pallas_call x2, Pallas kernels, spectral(): pl.pallas_call(spectral_kernel, grid=(modes,), in_specs=[pl.BlockSpec((co...  27 us
  transfers between devices with their start and end apart: 3, of which 2 were waited for; matrix products, arithmetic and copies ran while one was open for 3% of the time, Pallas kernels for 0%

profile of v1, /device:TPU:0, one launch (start us, length us, event | category | flops | bytes accessed | tf_op | source)
XLA Modules:
  0.0 353.8 jit_solution(7405634561020675580)
XLA Ops:
  0.6 0.0 copy-start
  0.6 2.2 copy.14
  2.9 1.5 copy.16
  4.3 6.3 %all-to-all-start = ((f32[4,2,4,64,256]{4,3,2,1,0:T(8,128)}), f32[4,2,4,64,256]{4,3,2,1,0:T(8,128)}, u32[]{:S(2)}, u32[]{:S(2)}) async-start(f32[4,2,4,64,256]{4,3,2,1,0:T(8,128)} %bitcast.22), calls=%async_computation | async-start | bytes 4194304 | tf_op jit(solution)/shard_map/all_to_all | solution.py:342
  10.7 0.0 copy-done
  10.7 0.1 constant_dynamic-slice_fusion
  10.8 1.0 fusion.24
  11.8 1.0 fusion.22
  12.8 1.0 fusion.20
  13.9 0.1 fusion.13
  14.0 3.8 %fusion.5 = (f32[1,4,256,256]{3,2,1,0:T(8,128)S(1)}, f32[1,4,256,256]{3,2,1,0:T(8,128)S(1)}) fusion(f32[4]{0:T(128)S(1)} %get-tuple-element.17, f32[256,256]{1,0:T(8,128)S(1)} %fusion.13, f32[4]{0:T(128)S(1)} %get-tuple-element.18, f32[4]{0:T(128)S(1)} %get-tuple-element.16), kind=kLoop, calls=%fused_computation.17 | loop fusion | flops 1310720 | bytes 2359344 | tf_op jit(solution)/shard_map/cos | solution.py:336
  17.8 1.5 maximum_multiply_fusion.rotor_ref
  19.3 0.3 fusion.3
  19.5 0.0 copy-start.1
  19.6 0.0 copy-start.3
  19.6 0.0 copy-start.5
  19.6 39.4 %all-to-all-done.x_ref = f32[4,2,4,64,256]{4,3,2,1,0:T(8,128)} async-done(((f32[4,2,4,64,256]{4,3,2,1,0:T(8,128)}), f32[4,2,4,64,256]{4,3,2,1,0:T(8,128)}, u32[]{:S(2)}, u32[]{:S(2)}) %all-to-all-start) | async-done | bytes 2097184 | tf_op jit(solution)/shard_map/all_to_all | solution.py:342
  59.0 13.8 %spectral.2 = f32[32,2,4,8,256]{4,3,2,1,0:T(8,128)} custom-call(f32[4,2,4,64,256]{4,3,2,1,0:T(8,128)} %all-to-all-done.x_ref, bf16[512,512]{1,0:T(8,128)(2,1)S(1)} %get-tuple-element.12.m1h, bf16[512,512]{1,0:T(8,128)(2,1)S(1)} %get-tuple-element.11.m1l, bf16[512,512]{1,0:T(8,128)(2,1)S(1)} %get-tuple-element.13.m2h, ...), custom_call_target="tpu_custom_call" | custom-call | tf_op jit(solution)/shard_map/spectral/pallas_call | solution.py:230
  72.8 0.0 copy-done.1
  72.8 0.0 copy-done.3
  72.8 0.0 copy-done.5
  72.8 0.0 copy-start.10
  72.8 0.0 copy-start.9
  72.8 3.7 %all-to-all-start.1 = ((f32[32,2,4,8,256]{4,3,2,1,0:T(8,128)}), f32[32,2,4,8,256]{4,3,2,1,0:T(8,128)S(1)}, u32[]{:S(2)}, u32[]{:S(2)}) async-start(f32[32,2,4,8,256]{4,3,2,1,0:T(8,128)} %spectral.2), calls=%async_computation.1 | async-start | bytes 4194304 | tf_op jit(solution)/shard_map/all_to_all | solution.py:346
  76.5 0.0 copy-done.10
  76.5 0.1 fusion.29.quartets
  76.6 48.7 %all-to-all-done.1 = f32[32,2,4,8,256]{4,3,2,1,0:T(8,128)S(1)} async-done(((f32[32,2,4,8,256]{4,3,2,1,0:T(8,128)}), f32[32,2,4,8,256]{4,3,2,1,0:T(8,128)S(1)}, u32[]{:S(2)}, u32[]{:S(2)}) %all-to-all-start.1) | async-done | bytes 2097184 | tf_op jit(solution)/shard_map/all_to_all | solution.py:346
  125.3 0.0 copy-done.9
  125.3 20.6 %kerr.2 = (f32[256,8,256]{2,1,0:T(8,128)S(1)}, f32[2,256,256]{2,1,0:T(8,128)S(1)}) custom-call(s32[4,1024]{1,0:T(4,128)S(1)} %fusion.29.quartets, f32[1024]{0:T(1024)S(1)} %copy-done.9, f32[256,8,256]{2,1,0:T(8,128)S(1)} %bitcast.23), custom_call_target="tpu_custom_call" | custom-call | tf_op jit(solution)/shard_map/kerr/pallas_call | solution.py:287
  145.8 0.0 copy-start.7
  145.8 0.8 copy-done.7
  146.6 52.7 %all_to_all.25.x_ref = f32[32,2,4,8,256]{4,3,2,1,0:T(8,128)} all-to-all(f32[32,2,4,8,256]{4,3,2,1,0:T(8,128)S(1)} %bitcast.26), channel_id=1, replica_groups=mesh['mode'=8,'tm'=4] {'tm','mode'}, dimensions={0} | all-to-all | bytes 4194304 | tf_op jit(solution)/shard_map/all_to_all | solution.py:353
  199.3 0.0 copy-done.2
  199.3 0.0 copy-done.6
  199.3 13.2 %spectral.3 = f32[32,2,4,8,256]{4,3,2,1,0:T(8,128)S(1)} custom-call(f32[32,2,4,8,256]{4,3,2,1,0:T(8,128)} %all_to_all.25.x_ref, bf16[512,512]{1,0:T(8,128)(2,1)S(1)} %copy-done.4, bf16[512,512]{1,0:T(8,128)(2,1)S(1)} %copy-done.2, bf16[512,512]{1,0:T(8,128)(2,1)S(1)} %copy-done.6, bf16[512,512]{1,0:T(8,128)(2,1)S(1)} %get-tuple-element.10.m2l, ...), custom_call_target="tpu_custom_call" | custom-call | tf_op jit(solution)/shard_map/spectral/pallas_call | solution.py:230
  212.5 52.2 %all_to_all.26 = f32[32,2,4,8,256]{4,3,2,1,0:T(8,128)S(1)} all-to-all(f32[32,2,4,8,256]{4,3,2,1,0:T(8,128)S(1)} %spectral.3), channel_id=1, replica_groups=mesh['mode'=8,'tm'=4] {'tm','mode'}, dimensions={0} | all-to-all | bytes 4194304 | tf_op jit(solution)/shard_map/all_to_all | solution.py:346
  264.7 20.6 %kerr.3 = (f32[256,8,256]{2,1,0:T(8,128)S(1)}, f32[2,256,256]{2,1,0:T(8,128)S(1)}) custom-call(s32[4,1024]{1,0:T(4,128)S(1)} %fusion.29.quartets, f32[1024]{0:T(1024)S(1)} %copy-done.9, f32[256,8,256]{2,1,0:T(8,128)S(1)} %bitcast.24), custom_call_target="tpu_custom_call" | custom-call | tf_op jit(solution)/shard_map/kerr/pallas_call | solution.py:287
  285.3 1.6 copy.12
  286.8 3.8 %all-to-all-start.4 = ((f32[4,8,2,4,8,256]{5,4,3,2,0,1:T(8,128)}), f32[4,8,2,4,8,256]{5,4,3,2,0,1:T(8,128)S(1)}, u32[]{:S(2)}, u32[]{:S(2)}) async-start(f32[4,8,2,4,8,256]{5,4,3,2,0,1:T(8,128)} %copy.12), calls=%async_computation.4 | async-start | bytes 4194304 | tf_op jit(solution)/shard_map/all_to_all | solution.py:355
  290.7 0.2 maximum_reduce_fusion
  290.9 0.2 reshape.181
  291.1 0.2 reduce_sum.19
  291.3 57.4 %psum.7 = f32[2,2,4,8,4]{4,3,2,1,0:T(8,128)S(1)} all-reduce(f32[2,2,4,8,4]{4,3,2,1,0:T(8,128)S(1)} %reduce_sum.19), channel_id=1, replica_groups=mesh['mode'=8,'tm'=4] {'mode','tm'}, use_global_device_ids=true, to_apply=%region_2.3 | all-reduce | flops 512 | bytes 4096 | tf_op jit(solution)/shard_map/psum | solution.py:360
  348.8 0.1 reshape.182
  348.8 0.6 fusion.34
  349.4 0.0 all-to-all-done.4
  349.4 1.6 copy.13
  351.1 2.7 reshape.180
  (10 shorter events, 0.1 us)
Async XLA Ops:
  0.6 10.1 %copy-start = (f32[3,16]{1,0:T(4,128)S(1)}, f32[3,16]{1,0:T(4,128)}, u32[]{:S(2)}) copy-start(f32[3,16]{1,0:T(4,128)} %param.5) | copy-start | bytes 580
  4.3 54.6 %all-to-all-start = ((f32[4,2,4,64,256]{4,3,2,1,0:T(8,128)}), f32[4,2,4,64,256]{4,3,2,1,0:T(8,128)}, u32[]{:S(2)}, u32[]{:S(2)}) async-start(f32[4,2,4,64,256]{4,3,2,1,0:T(8,128)} %bitcast.22), calls=%async_computation | async-start | bytes 4194304 | tf_op jit(solution)/shard_map/all_to_all | solution.py:342
  19.5 53.2 %copy-start.1 = (bf16[512,512]{1,0:T(8,128)(2,1)}, bf16[512,512]{1,0:T(8,128)(2,1)S(1)}, u32[]{:S(2)}) copy-start(bf16[512,512]{1,0:T(8,128)(2,1)S(1)} %get-tuple-element.11.m1l) | copy-start | bytes 1572868
  19.6 53.2 %copy-start.3 = (bf16[512,512]{1,0:T(8,128)(2,1)}, bf16[512,512]{1,0:T(8,128)(2,1)S(1)}, u32[]{:S(2)}) copy-start(bf16[512,512]{1,0:T(8,128)(2,1)S(1)} %get-tuple-element.12.m1h) | copy-start | bytes 1572868
  19.6 53.2 %copy-start.5 = (bf16[512,512]{1,0:T(8,128)(2,1)}, bf16[512,512]{1,0:T(8,128)(2,1)S(1)}, u32[]{:S(2)}) copy-start(bf16[512,512]{1,0:T(8,128)(2,1)S(1)} %get-tuple-element.13.m2h) | copy-start | bytes 1572868
  72.8 3.8 %copy-start.10 = (s32[4,1024]{1,0:T(4,128)S(1)}, s32[4,1024]{1,0:T(4,128)}, u32[]{:S(2)}) copy-start(s32[4,1024]{1,0:T(4,128)} %param.6) | copy-start | bytes 49156
  72.8 52.5 %copy-start.9 = (f32[1024]{0:T(1024)S(1)}, f32[1024]{0:T(1024)}, u32[]{:S(2)}) copy-start(f32[1024]{0:T(1024)} %weights.3) | copy-start | bytes 12292
  72.8 52.5 %all-to-all-start.1 = ((f32[32,2,4,8,256]{4,3,2,1,0:T(8,128)}), f32[32,2,4,8,256]{4,3,2,1,0:T(8,128)S(1)}, u32[]{:S(2)}, u32[]{:S(2)}) async-start(f32[32,2,4,8,256]{4,3,2,1,0:T(8,128)} %spectral.2), calls=%async_computation.1 | async-start | bytes 4194304 | tf_op jit(solution)/shard_map/all_to_all | solution.py:346
  145.8 0.8 copy-start.7
  146.6 52.7 %copy-start.2 = (bf16[512,512]{1,0:T(8,128)(2,1)S(1)}, bf16[512,512]{1,0:T(8,128)(2,1)}, u32[]{:S(2)}) copy-start(bf16[512,512]{1,0:T(8,128)(2,1)} %copy-done.1) | copy-start | bytes 1572868
  146.6 52.7 %copy-start.4 = (bf16[512,512]{1,0:T(8,128)(2,1)S(1)}, bf16[512,512]{1,0:T(8,128)(2,1)}, u32[]{:S(2)}) copy-start(bf16[512,512]{1,0:T(8,128)(2,1)} %copy-done.3) | copy-start | bytes 1572868
  146.6 52.7 %copy-start.6 = (bf16[512,512]{1,0:T(8,128)(2,1)S(1)}, bf16[512,512]{1,0:T(8,128)(2,1)}, u32[]{:S(2)}) copy-start(bf16[512,512]{1,0:T(8,128)(2,1)} %copy-done.5) | copy-start | bytes 1572868
  286.8 3.8 %copy-start.8 = (f32[2,256,256]{2,1,0:T(8,128)S(1)}, f32[2,256,256]{2,1,0:T(8,128)}, u32[]{:S(2)}) copy-start(f32[2,256,256]{2,1,0:T(8,128)} %copy-done.7) | copy-start | bytes 1572868
  286.8 62.6 %all-to-all-start.4 = ((f32[4,8,2,4,8,256]{5,4,3,2,0,1:T(8,128)}), f32[4,8,2,4,8,256]{5,4,3,2,0,1:T(8,128)S(1)}, u32[]{:S(2)}, u32[]{:S(2)}) async-start(f32[4,8,2,4,8,256]{5,4,3,2,0,1:T(8,128)} %copy.12), calls=%async_computation.4 | async-start | bytes 4194304 | tf_op jit(solution)/shard_map/all_to_all | solution.py:355

commit v2 on v1

--- a/solution.py
+++ b/solution.py
@@ -180,6 +180,7 @@
 
 
 UNROLL = 8
+CHAINS = 1
 
 
 def split(value):
@@ -240,36 +241,46 @@
     )(x, *tables, twist, rotor)
 
 
-def kerr_kernel(stride, quartets, weights, lin_ref, out_ref, err_ref, first_ref, acc_ref, mid_ref):
-    count = quartets.shape[1]
+def kerr_kernel(stride, quartets, weights, lin_ref, out_ref, err_ref, mid_ref, *accs):
+    chains = len(accs) // 2
+    count = weights.shape[0]
     unroll = UNROLL if count % UNROLL == 0 else 1
 
-    def evaluate(src, dst):
-        dst[...] = jnp.zeros_like(dst)
+    def evaluate(src, totals):
+        for total in totals:
+            total[...] = jnp.zeros_like(total)
 
         def chunk(c, carry):
             pending = []
             for u in range(unroll):
                 q = c * unroll + u
-                l, m, n = quartets[1, q], quartets[2, q], quartets[3, q]
+                l, m, n = quartets[4 * q + 1], quartets[4 * q + 2], quartets[4 * q + 3]
                 w = weights[q]
                 re, im = triple_product(
                     (src[l], src[l + stride]), (src[m], src[m + stride]), (src[n], src[n + stride])
                 )
-                pending.append((quartets[0, q], -w * im, w * re))
-            for p, re, im in pending:
-                dst[p] += re
-                dst[p + stride] += im
+                pending.append((quartets[4 * q], -w * im, w * re))
+            for u, (p, re, im) in enumerate(pending):
+                total = totals[u % chains]
+                total[p] += re
+                total[p + stride] += im
             return carry
 
         lax.fori_loop(0, count // unroll, chunk, 0)
 
-    evaluate(lin_ref, first_ref)
-    mid_ref[...] = lin_ref[...] + first_ref[...]
-    evaluate(mid_ref, acc_ref)
+    evaluate(lin_ref, accs[:chains])
+    first_ref = accs[0]
+
+    def combine(i, carry):
+        first_ref[i] = sum(total[i] for total in accs[:chains])
+        mid_ref[i] = lin_ref[i] + first_ref[i]
+        return carry
+
+    lax.fori_loop(0, lin_ref.shape[0], combine, 0, unroll=4)
+    evaluate(mid_ref, accs[chains:])
 
     def finish(i, carry):
-        first, second = first_ref[i], acc_ref[i]
+        first, second = first_ref[i], sum(total[i] for total in accs[chains:])
         new = lin_ref[i] + 0.5 * (first + second)
         estimate = 0.5 * (second - first)
         out_ref[i] = new
@@ -292,7 +303,7 @@
             jax.ShapeDtypeStruct(lin.shape, jnp.float32),
             jax.ShapeDtypeStruct((2, planes, lanes), jnp.float32),
         ],
-        scratch_shapes=[pltpu.VMEM(lin.shape, jnp.float32)] * 3,
+        scratch_shapes=[pltpu.VMEM(lin.shape, jnp.float32)] * (1 + 2 * CHAINS),
         compiler_params=pltpu.CompilerParams(vmem_limit_bytes=40 * 1024 * 1024),
         name="kerr",
     )(quartets, weights, lin)
@@ -308,7 +319,6 @@
     modes_all = modes_local * mode_ways
     rows = radix // devices
     tm_index = lax.axis_index("tm")
-    mode_index = lax.axis_index("mode")
 
     table_re, table_im = dft_tables(radix)
     m1 = jnp.concatenate(
@@ -336,7 +346,7 @@
     rotor = jnp.stack([jnp.cos(phase), jnp.sin(phase)]) * (1.0 / total_time)
 
     holder = quartets % modes_local // own * mode_ways + quartets // modes_local
-    planes = holder * (2 * own) + quartets % own
+    planes = (holder * (2 * own) + quartets % own).T.reshape(-1)
 
     state = field.reshape(2, tm_ways, own, time_local // radix, radix).transpose(1, 0, 2, 3, 4)
     state = lax.all_to_all(state, "tm", split_axis=0, concat_axis=0, tiled=True)
@@ -356,10 +366,11 @@
     out = state.transpose(2, 0, 3, 1, 4, 5).reshape(2, modes_local, time_local)
 
     norms = jnp.sum(jnp.stack(sums), axis=-1).reshape(STEPS, 2, tm_ways, mode_ways, 2, own)
-    norms = jnp.sum(norms, axis=4)
-    norms = lax.psum(norms, ("mode", "tm"))
-    norms = lax.dynamic_index_in_dim(norms, mode_index, axis=3, keepdims=False)
-    norms = norms.reshape(STEPS, 2, modes_local)
+    norms = jnp.sum(norms, axis=4).transpose(3, 0, 1, 2, 4).reshape(mode_ways, -1)
+    norms = jnp.broadcast_to(norms[:, None], (mode_ways, tm_ways, norms.shape[1]))
+    norms = norms.reshape(devices, 1, -1)
+    norms = lax.all_to_all(norms, ("mode", "tm"), split_axis=0, concat_axis=0, tiled=True)
+    norms = jnp.sum(norms, axis=0).reshape(STEPS, 2, modes_local)
     errors = jnp.sqrt(norms[:, 0] / (norms[:, 1] + epsilon))
     return (out, errors)
 

time: 354 us -> 327 us (0.924)
  blocking collectives: 162 us -> 105 us
  waiting for transfers between devices: 88.1 us -> 117 us
  Pallas kernels: 68.1 us -> 63.6 us
    psum x1 -> x0, blocking collectives: 57.4 us -> none  [shards(): norms = lax.psum(norms, ('mode', 'tm'))]
    all_to_all x1, waiting for transfers between devices: 0.01 us -> 25.8 us  [shards(): lax.all_to_all(state, 'mode', split_axis=1, concat_axis=1, tiled=True)]
    all_to_all x0 -> x1, waiting for transfers between devices: none -> 5.73 us  [shards(): lax.all_to_all(norms, ('mode', 'tm'), split_axis=0, concat_axis=0, tiled=...]
    pallas_call x2, Pallas kernels: 41.1 us -> 36.8 us  [kerr(): pl.pallas_call(functools.partial(kerr_kernel, stride), in_specs=[smem, sm...]
    all_to_all x0 -> x1, starting transfers between devices: none -> 3.66 us  [shards(): lax.all_to_all(norms, ('mode', 'tm'), split_axis=0, concat_axis=0, tiled=...]
  transfers between devices with their start and end apart: 3 -> 4, of which waited for: 2 -> 4; matrix products, arithmetic and copies ran while one was open for 3% -> 4% of each run, Pallas kernels for 0% -> 0%
where the time goes in v2:
time: 327 us
  waiting for transfers between devices  117 us (36%)
  blocking collectives  105 us (32%)
  Pallas kernels  63.6 us (19%)
  starting transfers between devices  17.3 us (5%)
  local copies, waits for them, and re-layouts  13.1 us (4%)
  other arithmetic  9.83 us (3%)
    all_to_all x2, blocking collectives, shards(): lax.all_to_all(state, ('tm', 'mode'), split_axis=0, concat_axis=0, tiled=...  105 us
    all_to_all x1, waiting for transfers between devices, shards(): lax.all_to_all(state, ('tm', 'mode'), split_axis=0, concat_axis=0, tiled=...  46.3 us
    all_to_all x1, waiting for transfers between devices, shards(): state = lax.all_to_all(state, 'tm', split_axis=0, concat_axis=0, tiled=True)  39.4 us
    pallas_call x2, Pallas kernels, kerr(): pl.pallas_call(functools.partial(kerr_kernel, stride), in_specs=[smem, sm...  36.8 us
    pallas_call x2, Pallas kernels, spectral(): pl.pallas_call(spectral_kernel, grid=(modes,), in_specs=[pl.BlockSpec((co...  26.9 us
    all_to_all x1, waiting for transfers between devices, shards(): lax.all_to_all(state, 'mode', split_axis=1, concat_axis=1, tiled=True)  25.8 us
  transfers between devices with their start and end apart: 4, of which 4 were waited for; matrix products, arithmetic and copies ran while one was open for 4% of the time, Pallas kernels for 0%

profile of v2, /device:TPU:0, one launch (start us, length us, event | category | flops | bytes accessed | tf_op | source)
XLA Modules:
  0.0 326.8 jit_solution(505043676764083640)
XLA Ops:
  0.6 0.0 copy-start
  0.6 2.2 copy.22
  2.9 1.5 copy.24
  4.3 6.3 %all-to-all-start = ((f32[4,2,4,64,256]{4,3,2,1,0:T(8,128)}), f32[4,2,4,64,256]{4,3,2,1,0:T(8,128)}, u32[]{:S(2)}, u32[]{:S(2)}) async-start(f32[4,2,4,64,256]{4,3,2,1,0:T(8,128)} %bitcast.27), calls=%async_computation | async-start | bytes 4194304 | tf_op jit(solution)/shard_map/all_to_all | solution.py:352
  10.7 0.0 copy-done
  10.7 0.1 constant_dynamic-slice_fusion
  10.8 1.0 fusion.24
  11.8 1.0 fusion.22
  12.8 1.0 fusion.20
  13.9 0.1 fusion.13
  14.0 3.8 %fusion.5 = (f32[1,4,256,256]{3,2,1,0:T(8,128)S(1)}, f32[1,4,256,256]{3,2,1,0:T(8,128)S(1)}) fusion(f32[4]{0:T(128)S(1)} %get-tuple-element.17, f32[256,256]{1,0:T(8,128)S(1)} %fusion.13, f32[4]{0:T(128)S(1)} %get-tuple-element.18, f32[4]{0:T(128)S(1)} %get-tuple-element.16), kind=kLoop, calls=%fused_computation.17 | loop fusion | flops 1310720 | bytes 2359344 | tf_op jit(solution)/shard_map/cos | solution.py:346
  17.8 1.5 maximum_multiply_fusion.rotor_ref
  19.3 0.3 fusion.3
  19.6 0.0 copy-start.1
  19.6 0.0 copy-start.3
  19.6 0.0 copy-start.5
  19.6 39.4 %all-to-all-done.x_ref = f32[4,2,4,64,256]{4,3,2,1,0:T(8,128)} async-done(((f32[4,2,4,64,256]{4,3,2,1,0:T(8,128)}), f32[4,2,4,64,256]{4,3,2,1,0:T(8,128)}, u32[]{:S(2)}, u32[]{:S(2)}) %all-to-all-start) | async-done | bytes 2097184 | tf_op jit(solution)/shard_map/all_to_all | solution.py:352
  59.0 13.9 %spectral.2 = f32[32,2,4,8,256]{4,3,2,1,0:T(8,128)} custom-call(f32[4,2,4,64,256]{4,3,2,1,0:T(8,128)} %all-to-all-done.x_ref, bf16[512,512]{1,0:T(8,128)(2,1)S(1)} %get-tuple-element.12.m1h, bf16[512,512]{1,0:T(8,128)(2,1)S(1)} %get-tuple-element.11.m1l, bf16[512,512]{1,0:T(8,128)(2,1)S(1)} %get-tuple-element.13.m2h, ...), custom_call_target="tpu_custom_call" | custom-call | tf_op jit(solution)/shard_map/spectral/pallas_call | solution.py:231
  72.9 0.0 copy-start.8
  72.9 0.0 copy-start.7
  72.9 3.7 %all-to-all-start.1 = ((f32[32,2,4,8,256]{4,3,2,1,0:T(8,128)}), f32[32,2,4,8,256]{4,3,2,1,0:T(8,128)S(1)}, u32[]{:S(2)}, u32[]{:S(2)}) async-start(f32[32,2,4,8,256]{4,3,2,1,0:T(8,128)} %spectral.2), calls=%async_computation.1 | async-start | bytes 4194304 | tf_op jit(solution)/shard_map/all_to_all | solution.py:356
  76.6 0.1 fusion.30
  76.7 1.0 copy.16
  77.7 1.3 reshape.184.quartets
  79.0 46.3 %all-to-all-done.1 = f32[32,2,4,8,256]{4,3,2,1,0:T(8,128)S(1)} async-done(((f32[32,2,4,8,256]{4,3,2,1,0:T(8,128)}), f32[32,2,4,8,256]{4,3,2,1,0:T(8,128)S(1)}, u32[]{:S(2)}, u32[]{:S(2)}) %all-to-all-start.1) | async-done | bytes 2097184 | tf_op jit(solution)/shard_map/all_to_all | solution.py:356
  125.4 18.4 %kerr.2 = (f32[256,8,256]{2,1,0:T(8,128)S(1)}, f32[2,256,256]{2,1,0:T(8,128)S(1)}) custom-call(s32[4096]{0:T(1024)S(1)} %reshape.184.quartets, f32[1024]{0:T(1024)S(1)} %copy-done.7, f32[256,8,256]{2,1,0:T(8,128)S(1)} %bitcast.28), custom_call_target="tpu_custom_call" | custom-call | tf_op jit(solution)/shard_map/kerr/pallas_call | solution.py:298
  143.8 52.7 %all_to_all.30.x_ref = f32[32,2,4,8,256]{4,3,2,1,0:T(8,128)} all-to-all(f32[32,2,4,8,256]{4,3,2,1,0:T(8,128)S(1)} %bitcast.31), channel_id=1, replica_groups=mesh['mode'=8,'tm'=4] {'tm','mode'}, dimensions={0} | all-to-all | bytes 4194304 | tf_op jit(solution)/shard_map/all_to_all | solution.py:363
  196.4 0.0 copy-done.2
  196.5 0.0 copy-done.6
  196.5 13.0 %spectral.3 = f32[32,2,4,8,256]{4,3,2,1,0:T(8,128)S(1)} custom-call(f32[32,2,4,8,256]{4,3,2,1,0:T(8,128)} %all_to_all.30.x_ref, bf16[512,512]{1,0:T(8,128)(2,1)S(1)} %copy-done.4, bf16[512,512]{1,0:T(8,128)(2,1)S(1)} %copy-done.2, bf16[512,512]{1,0:T(8,128)(2,1)S(1)} %copy-done.6, bf16[512,512]{1,0:T(8,128)(2,1)S(1)} %get-tuple-element.10.m2l, ...), custom_call_target="tpu_custom_call" | custom-call | tf_op jit(solution)/shard_map/spectral/pallas_call | solution.py:231
  209.5 52.2 %all_to_all.31 = f32[32,2,4,8,256]{4,3,2,1,0:T(8,128)S(1)} all-to-all(f32[32,2,4,8,256]{4,3,2,1,0:T(8,128)S(1)} %spectral.3), channel_id=1, replica_groups=mesh['mode'=8,'tm'=4] {'tm','mode'}, dimensions={0} | all-to-all | bytes 4194304 | tf_op jit(solution)/shard_map/all_to_all | solution.py:356
  261.6 18.4 %kerr.3 = (f32[256,8,256]{2,1,0:T(8,128)S(1)}, f32[2,256,256]{2,1,0:T(8,128)S(1)}) custom-call(s32[4096]{0:T(1024)S(1)} %reshape.184.quartets, f32[1024]{0:T(1024)S(1)} %copy-done.7, f32[256,8,256]{2,1,0:T(8,128)S(1)} %bitcast.29), custom_call_target="tpu_custom_call" | custom-call | tf_op jit(solution)/shard_map/kerr/pallas_call | solution.py:298
  280.0 0.2 maximum_reduce_fusion
  280.2 0.2 reshape.190
  280.5 0.2 reduce_sum.28
  280.6 0.2 copy.20
  280.8 0.1 copy.21
  280.9 0.6 broadcast_in_dim.5
  281.5 3.7 %all-to-all-start.5 = ((f32[32,1,64]{2,1,0:T(1,128)}), f32[32,1,64]{2,1,0:T(1,128)S(1)}, u32[]{:S(2)}, u32[]{:S(2)}) async-start(f32[32,1,64]{2,1,0:T(1,128)} %bitcast.14), calls=%async_computation.5 | async-start | bytes 32768 | tf_op jit(solution)/shard_map/all_to_all | solution.py:372
  285.2 1.5 copy.18
  286.6 5.7 %all-to-all-done.5 = f32[32,1,64]{2,1,0:T(1,128)S(1)} async-done(((f32[32,1,64]{2,1,0:T(1,128)}), f32[32,1,64]{2,1,0:T(1,128)S(1)}, u32[]{:S(2)}, u32[]{:S(2)}) %all-to-all-start.5) | async-done | bytes 8224 | tf_op jit(solution)/shard_map/all_to_all | solution.py:372
  292.4 3.6 %all-to-all-start.4 = ((f32[4,8,2,4,8,256]{5,4,3,2,0,1:T(8,128)}), f32[4,8,2,4,8,256]{5,4,3,2,0,1:T(8,128)S(1)}, u32[]{:S(2)}, u32[]{:S(2)}) async-start(f32[4,8,2,4,8,256]{5,4,3,2,0,1:T(8,128)} %copy.18), calls=%async_computation.4 | async-start | bytes 4194304 | tf_op jit(solution)/shard_map/all_to_all | solution.py:365
  296.0 0.1 reduce_sum.29
  296.0 0.1 reshape.192
  296.1 0.6 fusion.35
  296.7 25.8 %all-to-all-done.4 = f32[4,8,2,4,8,256]{5,4,3,2,0,1:T(8,128)S(1)} async-done(((f32[4,8,2,4,8,256]{5,4,3,2,0,1:T(8,128)}), f32[4,8,2,4,8,256]{5,4,3,2,0,1:T(8,128)S(1)}, u32[]{:S(2)}, u32[]{:S(2)}) %all-to-all-start.4) | async-done | bytes 2097184 | tf_op jit(solution)/shard_map/all_to_all | solution.py:365
  322.5 1.6 copy.19
  324.1 2.7 reshape.189
  (12 shorter events, 0.1 us)
Async XLA Ops:
  0.6 10.1 %copy-start = (f32[3,16]{1,0:T(4,128)S(1)}, f32[3,16]{1,0:T(4,128)}, u32[]{:S(2)}) copy-start(f32[3,16]{1,0:T(4,128)} %param.5) | copy-start | bytes 580
  4.3 54.6 %all-to-all-start = ((f32[4,2,4,64,256]{4,3,2,1,0:T(8,128)}), f32[4,2,4,64,256]{4,3,2,1,0:T(8,128)}, u32[]{:S(2)}, u32[]{:S(2)}) async-start(f32[4,2,4,64,256]{4,3,2,1,0:T(8,128)} %bitcast.27), calls=%async_computation | async-start | bytes 4194304 | tf_op jit(solution)/shard_map/all_to_all | solution.py:352
  19.6 53.3 %copy-start.1 = (bf16[512,512]{1,0:T(8,128)(2,1)}, bf16[512,512]{1,0:T(8,128)(2,1)S(1)}, u32[]{:S(2)}) copy-start(bf16[512,512]{1,0:T(8,128)(2,1)S(1)} %get-tuple-element.11.m1l) | copy-start | bytes 1572868
  19.6 53.3 %copy-start.3 = (bf16[512,512]{1,0:T(8,128)(2,1)}, bf16[512,512]{1,0:T(8,128)(2,1)S(1)}, u32[]{:S(2)}) copy-start(bf16[512,512]{1,0:T(8,128)(2,1)S(1)} %get-tuple-element.12.m1h) | copy-start | bytes 1572868
  19.6 53.3 %copy-start.5 = (bf16[512,512]{1,0:T(8,128)(2,1)}, bf16[512,512]{1,0:T(8,128)(2,1)S(1)}, u32[]{:S(2)}) copy-start(bf16[512,512]{1,0:T(8,128)(2,1)S(1)} %get-tuple-element.13.m2h) | copy-start | bytes 1572868
  72.9 3.7 %copy-start.8 = (s32[4,1024]{1,0:T(4,128)S(1)}, s32[4,1024]{1,0:T(4,128)}, u32[]{:S(2)}) copy-start(s32[4,1024]{1,0:T(4,128)} %param.6) | copy-start | bytes 49156
  72.9 52.5 %copy-start.7 = (f32[1024]{0:T(1024)S(1)}, f32[1024]{0:T(1024)}, u32[]{:S(2)}) copy-start(f32[1024]{0:T(1024)} %weights.3) | copy-start | bytes 12292
  72.9 52.5 %all-to-all-start.1 = ((f32[32,2,4,8,256]{4,3,2,1,0:T(8,128)}), f32[32,2,4,8,256]{4,3,2,1,0:T(8,128)S(1)}, u32[]{:S(2)}, u32[]{:S(2)}) async-start(f32[32,2,4,8,256]{4,3,2,1,0:T(8,128)} %spectral.2), calls=%async_computation.1 | async-start | bytes 4194304 | tf_op jit(solution)/shard_map/all_to_all | solution.py:356
  143.7 52.7 %copy-start.2 = (bf16[512,512]{1,0:T(8,128)(2,1)S(1)}, bf16[512,512]{1,0:T(8,128)(2,1)}, u32[]{:S(2)}) copy-start(bf16[512,512]{1,0:T(8,128)(2,1)} %copy-done.1) | copy-start | bytes 1572868
  143.7 52.7 %copy-start.4 = (bf16[512,512]{1,0:T(8,128)(2,1)S(1)}, bf16[512,512]{1,0:T(8,128)(2,1)}, u32[]{:S(2)}) copy-start(bf16[512,512]{1,0:T(8,128)(2,1)} %copy-done.3) | copy-start | bytes 1572868
  143.8 52.7 %copy-start.6 = (bf16[512,512]{1,0:T(8,128)(2,1)S(1)}, bf16[512,512]{1,0:T(8,128)(2,1)}, u32[]{:S(2)}) copy-start(bf16[512,512]{1,0:T(8,128)(2,1)} %copy-done.5) | copy-start | bytes 1572868
  281.5 10.9 %all-to-all-start.5 = ((f32[32,1,64]{2,1,0:T(1,128)}), f32[32,1,64]{2,1,0:T(1,128)S(1)}, u32[]{:S(2)}, u32[]{:S(2)}) async-start(f32[32,1,64]{2,1,0:T(1,128)} %bitcast.14), calls=%async_computation.5 | async-start | bytes 32768 | tf_op jit(solution)/shard_map/all_to_all | solution.py:372
  292.4 30.2 %all-to-all-start.4 = ((f32[4,8,2,4,8,256]{5,4,3,2,0,1:T(8,128)}), f32[4,8,2,4,8,256]{5,4,3,2,0,1:T(8,128)S(1)}, u32[]{:S(2)}, u32[]{:S(2)}) async-start(f32[4,8,2,4,8,256]{5,4,3,2,0,1:T(8,128)} %copy.18), calls=%async_computation.4 | async-start | bytes 4194304 | tf_op jit(solution)/shard_map/all_to_all | solution.py:365
